TPU v7x, 32 devices: a whole 2x2x4 slice. The times are simulated.
32 devices in a mesh: inl: 4 (over z), xln: 8 (over y, x, core).
Axes of the slice: x: 2, y: 2, z: 4, core: 2. Of those that a mesh axis runs over, the one named last changes fastest.
Arguments:
- noisy: float32 [128, 256, 512], P('inl', 'xln'), may hold values from -6 to 6
- bound: float32 [128, 256, 512], P('inl', 'xln'), may hold values from 0.05 to 0.5
Outputs:
- denoised: float32 [128, 256, 512], P('inl', 'xln')
- dual: float32 [3, 128, 256, 512], P(None, 'inl', 'xln')
- norms: float32 [2, 2], replicated
All inputs are finite; a program needn't handle non-finite values.
Results may differ from a plain program's by a relative error of at most 0.0001.
Values sent between devices are 32-bit elements; how exact they have to be, the bound alone decides.
A program may use at most 64 MiB of HBM per device.

v0:
```python
import functools

import jax
import jax.numpy as jnp
from jax import lax
from jax.experimental import pallas as pl
from jax.experimental.pallas import tpu as pltpu
from jax.sharding import PartitionSpec as P

SIGMA = 0.28
TAU = 0.28
GAIN = TAU / (1.0 + TAU)


def clip(value, limit):
    return jnp.minimum(jnp.maximum(value, -limit), limit)


def fold(square):
    rows, lanes = square.shape
    total = square[0:8]
    for at in range(8, rows, 8):
        total = total + square[at : at + 8]
    part = total[:, 0:128]
    for at in range(128, lanes, 128):
        part = part + total[:, at : at + 128]
    return part


def greeted(axis, count):
    return [k for k in range(1, count) if axis == "xln" or count > 4 or k in (1, count - 1)]


def split(value, dim, size):
    return [lax.slice_in_dim(value, at, at + size, axis=dim) for at in range(0, value.shape[dim], size)]


def ahead(value, dim):
    size = (8, 128)[dim]
    parts = split(value, dim, size)
    turned = [pltpu.roll(part, size - 1, dim) for part in parts]
    edge = lax.broadcasted_iota(jnp.int32, parts[0].shape, dim) == size - 1
    after = turned[1:] + [parts[-1]]
    return jnp.concatenate([jnp.where(edge, a, t) for a, t in zip(after, turned)], axis=dim)


def behind(value, dim):
    size = (8, 128)[dim]
    turned = [pltpu.roll(part, 1, dim) for part in split(value, dim, size)]
    edge = lax.broadcasted_iota(jnp.int32, turned[0].shape, dim) == 0
    before = [jnp.zeros_like(turned[0])] + turned[:-1]
    return jnp.concatenate([jnp.where(edge, a, t) for a, t in zip(before, turned)], axis=dim)


def kernel(
    ni_dev, nx_dev,
    noisy, bound, out, dual, norms,
    n, b, v, step,
    nx_first, nx_last, bx_last, nx_next, nx_prev, bx_prev,
    vx_first, vx_last, vx_next, vx_prev, dx_prev, dx_edge, di_prev,
    mine, others_x, others_i,
    load_sem, send_sem, recv_sem, xs_sem, xr_sem, is_sem, ir_sem,
):
    ni, nx, nz = noisy.shape
    top, end = ni, ni + 1
    my_i, my_x = lax.axis_index("inl"), lax.axis_index("xln")

    loads = []

    def load(src, dst):
        copy = pltpu.make_async_copy(src, dst, load_sem.at[len(loads)])
        copy.start()
        loads.append(copy)

    load(noisy.at[pl.ds(ni - 1, 1)], n.at[pl.ds(top, 1)])
    load(bound.at[pl.ds(ni - 1, 1)], b.at[pl.ds(top, 1)])
    load(noisy.at[pl.ds(0, 1)], n.at[pl.ds(1, 1)])
    load(noisy.at[pl.ds(1, ni - 2)], n.at[pl.ds(2, ni - 2)])
    load(bound.at[pl.ds(0, ni - 1)], b.at[pl.ds(1, ni - 1)])

    barrier = pltpu.get_barrier_semaphore()
    for axis, me, count in (("inl", my_i, ni_dev), ("xln", my_x, nx_dev)):
        for k in greeted(axis, count):
            pl.semaphore_signal(
                barrier, inc=1, device_id={axis: lax.rem(me + k, count)},
                device_id_type=pl.DeviceIdType.MESH,
            )
    pl.semaphore_wait(barrier, len(greeted("inl", ni_dev)) + len(greeted("xln", nx_dev)))

    sent = []

    def send(slot, src, dst, axis, forward):
        me, count = (my_i, ni_dev) if axis == "inl" else (my_x, nx_dev)
        target = lax.rem(me + (1 if forward else count - 1), count)
        copy = pltpu.make_async_remote_copy(
            src_ref=src, dst_ref=dst, send_sem=send_sem.at[slot], recv_sem=recv_sem.at[slot],
            device_id={axis: target}, device_id_type=pl.DeviceIdType.MESH,
        )
        not_last, not_first = me < count - 1, me > 0
        can_send, can_recv = (not_last, not_first) if forward else (not_first, not_last)

        @pl.when(can_send)
        def _():
            copy.start()

        sent.append((copy, can_send))

        def arrive(fill):
            @pl.when(can_recv)
            def _():
                copy.wait_recv()

            @pl.when(jnp.logical_not(can_recv))
            def _():
                fill()

        return arrive

    def setter(dst, src):
        def fill():
            dst[...] = src[...]

        return fill

    loads[0].wait()
    got_n_prev = send(0, n.at[top], n.at[0], "inl", True)
    loads[1].wait()
    got_b_prev = send(1, b.at[top], b.at[0], "inl", True)
    loads[2].wait()
    got_n_next = send(2, n.at[1], n.at[end], "inl", False)
    loads[3].wait()
    nx_last[...] = n[1:end, nx - 1, :]
    got_nx_prev = send(3, nx_last, nx_prev, "xln", True)
    nx_first[...] = n[1:end, 0, :]
    got_nx_next = send(5, nx_first, nx_next, "xln", False)
    loads[4].wait()
    bx_last[...] = b[1:end, nx - 1, :]
    got_bx_prev = send(4, bx_last, bx_prev, "xln", True)

    step[...] = jnp.zeros_like(step)

    def squares(oi, ox, oz):
        return fold(oi * oi + ox * ox + oz * oz)

    def pass_one(i, d1):
        here, limit = n[i + 1], b[i + 1]
        di = clip(SIGMA * (n[i + 2] - here), limit)
        dx = clip(SIGMA * (ahead(here, 0) - here), limit)
        dz = clip(SIGMA * (ahead(here, 1) - here), limit)
        dual[0, i] = di
        dual[1, i] = dx
        dual[2, i] = dz
        div = di - step[...]
        div = div + (dx - behind(dx, 0))
        div = div + (dz - behind(dz, 1))
        step[...] = di
        v[i + 1] = here + (2.0 * GAIN) * div
        return d1 + squares(di, dx, dz)

    zero = jnp.zeros((8, 128), jnp.float32)
    d1 = lax.fori_loop(0, ni - 1, pass_one, zero)
    here, limit = n[top], b[top]
    dx = clip(SIGMA * (ahead(here, 0) - here), limit)
    dz = clip(SIGMA * (ahead(here, 1) - here), limit)
    dual[1, ni - 1] = dx
    dual[2, ni - 1] = dz
    div = (dx - behind(dx, 0)) - step[...]
    div = div + (dz - behind(dz, 1))
    v[top] = here + (2.0 * GAIN) * div
    d1 = d1 + fold(dx * dx + dz * dz)

    got_nx_prev(setter(nx_prev, nx_first))
    got_bx_prev(setter(bx_prev, bx_last))
    got_nx_next(setter(nx_next, nx_last))
    dx_last = clip(SIGMA * (nx_next[...] - nx_last[...]), bx_last[...])
    dxp = clip(SIGMA * (nx_first[...] - nx_prev[...]), bx_prev[...])
    dual[1, :, nx - 1, :] = dx_last
    dx_prev[...] = dxp
    dx_edge[...] = dx_last
    v[1:end, nx - 1, :] = v[1:end, nx - 1, :] + (2.0 * GAIN) * dx_last
    v[1:end, 0, :] = v[1:end, 0, :] - (2.0 * GAIN) * dxp

    got_n_prev(setter(n.at[0], n.at[1]))
    got_b_prev(setter(b.at[0], b.at[1]))
    got_n_next(setter(n.at[end], n.at[top]))
    di_last = clip(SIGMA * (n[end] - n[top]), b[top])
    dip = clip(SIGMA * (n[1] - n[0]), b[0])
    dual[0, ni - 1] = di_last
    di_prev[...] = dip
    v[top] = v[top] + (2.0 * GAIN) * di_last
    v[1] = v[1] - (2.0 * GAIN) * dip
    got_v_prev = send(6, v.at[top], v.at[0], "inl", True)
    got_v_next = send(7, v.at[1], v.at[end], "inl", False)
    vx_last[...] = v[1:end, nx - 1, :]
    got_vx_prev = send(8, vx_last, vx_prev, "xln", True)
    vx_first[...] = v[1:end, 0, :]
    got_vx_next = send(9, vx_first, vx_next, "xln", False)
    d1 = d1 + fold(di_last * di_last) + fold(dx_last * dx_last)

    row = lax.broadcasted_iota(jnp.int32, (8, nz), 0)

    def inner_rows(value):
        parts = split(value, 0, 8)
        parts[0] = jnp.where(row == 0, 0.0, parts[0])
        parts[-1] = jnp.where(row == 7, 0.0, parts[-1])
        return jnp.concatenate(parts, axis=0)

    def pass_two(i, sums):
        p1, p2, d2 = sums
        here, limit, base = v[i + 1], b[i + 1], n[i + 1]
        oi, ox, oz = dual[0, i], dual[1, i], dual[2, i]
        di = clip(oi + SIGMA * (v[i + 2] - here), limit)
        dx = clip(ox + SIGMA * (ahead(here, 0) - here), limit)
        dz = clip(oz + SIGMA * (ahead(here, 1) - here), limit)
        dual[0, i] = di
        dual[1, i] = dx
        dual[2, i] = dz
        div = di - step[...]
        div = div + (dx - behind(dx, 0))
        div = div + (dz - behind(dz, 1))
        step[...] = di
        half = 0.5 * (here - base)
        change = GAIN * (div - half)
        out[i] = base + half + change
        inner = inner_rows(change)
        return (
            p1 + fold(half * half),
            p2 + fold(inner * inner),
            d2 + squares(di - oi, dx - ox, dz - oz),
        )

    step[...] = clip(dual[0, 0] + SIGMA * (v[2] - v[1]), b[1])
    sums = lax.fori_loop(1, ni - 1, pass_two, (zero,) * 3)

    got_v_next(setter(v.at[end], v.at[top]))
    sums = pass_two(ni - 1, sums)
    got_v_prev(setter(v.at[0], v.at[1]))
    step[...] = clip(di_prev[...] + SIGMA * (v[1] - v[0]), b[0])
    p1, p2, d2 = pass_two(0, sums)

    got_vx_prev(setter(vx_prev, vx_first))
    got_vx_next(setter(vx_next, vx_last))
    was = dx_edge[...]
    dx_last = clip(was + SIGMA * (vx_next[...] - vx_last[...]), bx_last[...])
    dual[1, :, nx - 1, :] = dx_last
    moved = dx_last - was
    d2 = d2 + fold(moved * moved)
    u_last = out[:, nx - 1, :] + GAIN * moved
    out[:, nx - 1, :] = u_last
    dxp = clip(dx_prev[...] + SIGMA * (vx_first[...] - vx_prev[...]), bx_prev[...])
    u_first = out[:, 0, :] - GAIN * dxp
    out[:, 0, :] = u_first
    change = u_last - (nx_last[...] + 0.5 * (vx_last[...] - nx_last[...]))
    p2 = p2 + fold(change * change)
    change = u_first - (nx_first[...] + 0.5 * (vx_first[...] - nx_first[...]))
    p2 = p2 + fold(change * change)

    for k, part in enumerate((p1, d1, p2, d2)):
        mine[0, k : k + 1] = jnp.sum(part, axis=0, keepdims=True)

    def reduce(count, me, axis, source, others, ss, rs):
        copies = []
        for k in range(1, count):
            copy = pltpu.make_async_remote_copy(
                src_ref=source, dst_ref=others.at[k - 1],
                send_sem=ss.at[k - 1], recv_sem=rs.at[k - 1],
                device_id={axis: lax.rem(me + k, count)}, device_id_type=pl.DeviceIdType.MESH,
            )
            copy.start()
            copies.append(copy)
        total = source[...]
        for copy in copies:
            copy.wait_recv()
        for k in range(count - 1):
            total = total + others[k]
        return total, copies

    total, copies_x = reduce(nx_dev, my_x, "xln", mine.at[0], others_x, xs_sem, xr_sem)
    mine[1] = total
    total, copies_i = reduce(ni_dev, my_i, "inl", mine.at[1], others_i, is_sem, ir_sem)
    at = 2 * lax.broadcasted_iota(jnp.int32, (2, 2), 0) + lax.broadcasted_iota(jnp.int32, (2, 2), 1)
    result = jnp.zeros((2, 2), jnp.float32)
    for k in range(4):
        result = jnp.where(at == k, jnp.sum(total[k : k + 1], keepdims=True), result)
    norms[...] = jnp.sqrt(result)

    for copy in copies_x + copies_i:
        copy.wait_send()
    for copy, can_send in sent:
        @pl.when(can_send)
        def _():
            copy.wait_send()


def put_out(out_held, dual_held, norms_held, out, dual, norms, sems):
    half = out.shape[0] // 2
    pairs = [(norms_held, norms)]
    for at in (0, half):
        part = pl.ds(at, half)
        pairs.append((out_held.at[part], out.at[part]))
        for axis in range(3):
            pairs.append((dual_held.at[axis, part], dual.at[axis, part]))
    copies = [pltpu.make_async_copy(src, dst, sems.at[k]) for k, (src, dst) in enumerate(pairs)]
    for copy in copies:
        copy.start()
    for copy in copies:
        copy.wait()


def per_device(noisy, bound):
    ni, nx, nz = noisy.shape
    ni_dev, nx_dev = lax.axis_size("inl"), lax.axis_size("xln")
    f32 = jnp.float32
    face = pltpu.VMEM((ni, nz), f32)
    slab = pltpu.VMEM((nx, nz), f32)
    dma = pltpu.SemaphoreType.DMA
    volume = 4 * ni * nx * nz
    noisy = pltpu.with_memory_space_constraint(noisy, pltpu.HBM)
    bound = pltpu.with_memory_space_constraint(bound, pltpu.HBM)
    held = pl.pallas_call(
        functools.partial(kernel, ni_dev, nx_dev),
        out_shape=(
            pltpu.VMEM((ni, nx, nz), f32),
            pltpu.VMEM((3, ni, nx, nz), f32),
            pltpu.VMEM((2, 2), f32),
        ),
        in_specs=[pl.BlockSpec(memory_space=pltpu.HBM)] * 2,
        out_specs=(
            pl.BlockSpec(memory_space=pltpu.VMEM),
            pl.BlockSpec(memory_space=pltpu.VMEM),
            pl.BlockSpec(memory_space=pltpu.VMEM),
        ),
        scratch_shapes=[
            pltpu.VMEM((ni + 2, nx, nz), f32),
            pltpu.VMEM((ni + 1, nx, nz), f32),
            pltpu.VMEM((ni + 2, nx, nz), f32),
            slab,
            *([face] * 12),
            slab,
            pltpu.VMEM((2, 4, 128), f32),
            pltpu.VMEM((nx_dev - 1, 4, 128), f32),
            pltpu.VMEM((ni_dev - 1, 4, 128), f32),
            dma((5,)), dma((10,)), dma((10,)),
            dma((nx_dev - 1,)), dma((nx_dev - 1,)), dma((ni_dev - 1,)), dma((ni_dev - 1,)),
        ],
        compiler_params=pltpu.CompilerParams(
            collective_id=0, has_side_effects=True, vmem_limit_bytes=24 * 1024 * 1024
        ),
        cost_estimate=pl.CostEstimate(
            flops=80 * ni * nx * nz, bytes_accessed=6 * volume, transcendentals=0
        ),
        name="denoise",
    )(noisy, bound)
    in_vmem = pl.BlockSpec(memory_space=pltpu.VMEM)
    in_hbm = pl.BlockSpec(memory_space=pltpu.HBM)
    return pl.pallas_call(
        put_out,
        out_shape=(
            jax.ShapeDtypeStruct((ni, nx, nz), f32),
            jax.ShapeDtypeStruct((3, ni, nx, nz), f32),
            jax.ShapeDtypeStruct((2, 2), f32),
        ),
        in_specs=[in_vmem] * 3,
        out_specs=(in_hbm,) * 3,
        scratch_shapes=[dma((9,))],
        compiler_params=pltpu.CompilerParams(vmem_limit_bytes=1024 * 1024),
        cost_estimate=pl.CostEstimate(flops=0, bytes_accessed=4 * volume, transcendentals=0),
        name="put_out",
    )(*held)


def solution(mesh):
    in_specs = (P("inl", "xln", None), P("inl", "xln", None))
    out_specs = (P("inl", "xln", None), P(None, "inl", "xln", None), P())
    return jax.shard_map(
        per_device, mesh=mesh, in_specs=in_specs, out_specs=out_specs, check_vma=False
    )
```

profile of v0, /device:TPU:0, one launch (start us, length us, event | category | flops | bytes accessed | tf_op | source)
XLA Modules:
  0.0 29.0 jit_solution(9438701532192778743)
XLA Ops:
  0.6 25.0 %denoise.1 = (f32[32,32,512]{2,1,0:T(8,128)S(1)}, f32[3,32,32,512]{3,2,1,0:T(8,128)S(1)}, f32[2,2]{1,0:T(2,128)S(1)}) custom-call(f32[32,32,512]{2,1,0:T(8,128)} %noisy.1, f32[32,32,512]{2,1,0:T(8,128)} %bound.1), custom_call_target="tpu_custom_call" | custom-call | flops 41943040 | bytes 12582912 | tf_op jit(solution)/shard_map/denoise/pallas_call | solution.py:320
  25.7 3.4 %put_out.1 = (f32[32,32,512]{2,1,0:T(8,128)}, f32[3,32,32,512]{3,2,1,0:T(8,128)}, f32[2,2]{1,0:T(2,128)}) custom-call(f32[32,32,512]{2,1,0:T(8,128)S(1)} %get-tuple-element.6.out_held, f32[3,32,32,512]{3,2,1,0:T(8,128)S(1)} %get-tuple-element.7.dual_held, f32[2,2]{1,0:T(2,128)S(1)} %get-tuple-element.8.norms_held), custom_call_target="tpu_custom_call" | custom-call | bytes 8388608 | tf_op jit(solution)/shard_map/put_out/pallas_call | solution.py:356
where the time goes:
time: 29.2 us; the launch traced here: 29 us
  Pallas kernels  28.4 us (97%)
  between operations  0.64 us (2%)
    pallas_call x1, Pallas kernels, per_device(): pl.pallas_call(functools.partial(kernel, ni_dev, nx_dev), out_shape=(pltp...  25 us
    pallas_call x1, Pallas kernels, per_device(): pl.pallas_call(put_out, out_shape=(jax.ShapeDtypeStruct((ni, nx, nz), f32...  3.38 us

commit v1 on v0

--- a/solution.py
+++ b/solution.py
@@ -27,8 +27,36 @@
     return part
 
 
-def greeted(axis, count):
-    return [k for k in range(1, count) if axis == "xln" or count > 4 or k in (1, count - 1)]
+def gather_lanes(rows):
+    lane = lax.broadcasted_iota(jnp.int32, (1, 128), 1)
+    result = jnp.zeros((1, 128), jnp.float32)
+    for k, row in enumerate(rows):
+        result = jnp.where(lane == k, jnp.sum(row, axis=1, keepdims=True), result)
+    return result
+
+
+def one_stage(ni_dev, nx_dev):
+    return ni_dev <= 4 and ni_dev * nx_dev <= 32
+
+
+def reduction(ni_dev, nx_dev):
+    everyone = [(di, dx) for di in range(ni_dev) for dx in range(nx_dev) if di or dx]
+    if one_stage(ni_dev, nx_dev):
+        return [everyone]
+    return [[peer for peer in everyone if peer[0] == 0], [peer for peer in everyone if peer[1] == 0]]
+
+
+def stepped(start, stop, body, carry, unroll=4):
+    def group(k, carry):
+        for at in range(unroll):
+            carry = body(start + k * unroll + at, carry)
+        return carry
+
+    whole = (stop - start) // unroll
+    carry = lax.fori_loop(0, whole, group, carry)
+    for i in range(start + whole * unroll, stop):
+        carry = body(i, carry)
+    return carry
 
 
 def split(value, dim, size):
@@ -58,8 +86,8 @@
     n, b, v, step,
     nx_first, nx_last, bx_last, nx_next, nx_prev, bx_prev,
     vx_first, vx_last, vx_next, vx_prev, dx_prev, dx_edge, di_prev,
-    mine, others_x, others_i,
-    load_sem, send_sem, recv_sem, xs_sem, xr_sem, is_sem, ir_sem,
+    mine, others,
+    load_sem, send_sem, recv_sem, give_sem, take_sem,
 ):
     ni, nx, nz = noisy.shape
     top, end = ni, ni + 1
@@ -79,13 +107,27 @@
     load(bound.at[pl.ds(0, ni - 1)], b.at[pl.ds(1, ni - 1)])
 
     barrier = pltpu.get_barrier_semaphore()
-    for axis, me, count in (("inl", my_i, ni_dev), ("xln", my_x, nx_dev)):
-        for k in greeted(axis, count):
-            pl.semaphore_signal(
-                barrier, inc=1, device_id={axis: lax.rem(me + k, count)},
-                device_id_type=pl.DeviceIdType.MESH,
-            )
-    pl.semaphore_wait(barrier, len(greeted("inl", ni_dev)) + len(greeted("xln", nx_dev)))
+    stages = reduction(ni_dev, nx_dev)
+
+    def at(di, dx):
+        return {"inl": lax.rem(my_i + di, ni_dev), "xln": lax.rem(my_x + dx, nx_dev)}
+
+    greeted = 0
+    for di in range(1 - ni_dev, ni_dev):
+        for dx in range(nx_dev):
+            if (di == 0 and dx == 0) or not (abs(di) <= 1 and (one_stage(ni_dev, nx_dev) or di * dx == 0) or (dx == 0 and not one_stage(ni_dev, nx_dev))):
+                continue
+            exists = jnp.logical_and(my_i + di >= 0, my_i + di < ni_dev)
+            greeted = greeted + exists.astype(jnp.int32)
+
+            @pl.when(exists)
+            def _():
+                pl.semaphore_signal(
+                    barrier, inc=1,
+                    device_id={"inl": my_i + di, "xln": lax.rem(my_x + dx, nx_dev)},
+                    device_id_type=pl.DeviceIdType.MESH,
+                )
+    pl.semaphore_wait(barrier, greeted)
 
     sent = []
 
@@ -158,7 +200,7 @@
         return d1 + squares(di, dx, dz)
 
     zero = jnp.zeros((8, 128), jnp.float32)
-    d1 = lax.fori_loop(0, ni - 1, pass_one, zero)
+    d1 = stepped(0, ni - 1, pass_one, zero)
     here, limit = n[top], b[top]
     dx = clip(SIGMA * (ahead(here, 0) - here), limit)
     dz = clip(SIGMA * (ahead(here, 1) - here), limit)
@@ -230,7 +272,7 @@
         )
 
     step[...] = clip(dual[0, 0] + SIGMA * (v[2] - v[1]), b[1])
-    sums = lax.fori_loop(1, ni - 1, pass_two, (zero,) * 3)
+    sums = stepped(1, ni - 1, pass_two, (zero,) * 3)
 
     got_v_next(setter(v.at[end], v.at[top]))
     sums = pass_two(ni - 1, sums)
@@ -255,36 +297,25 @@
     change = u_first - (nx_first[...] + 0.5 * (vx_first[...] - nx_first[...]))
     p2 = p2 + fold(change * change)
 
-    for k, part in enumerate((p1, d1, p2, d2)):
-        mine[0, k : k + 1] = jnp.sum(part, axis=0, keepdims=True)
-
-    def reduce(count, me, axis, source, others, ss, rs):
-        copies = []
-        for k in range(1, count):
+    total = gather_lanes([jnp.sum(part, axis=0, keepdims=True) for part in (p1, d1, p2, d2)])
+    copies = []
+    for stage, peers in enumerate(stages):
+        mine[stage] = total
+        first = len(copies)
+        for k, (di, dx) in enumerate(peers, first):
             copy = pltpu.make_async_remote_copy(
-                src_ref=source, dst_ref=others.at[k - 1],
-                send_sem=ss.at[k - 1], recv_sem=rs.at[k - 1],
-                device_id={axis: lax.rem(me + k, count)}, device_id_type=pl.DeviceIdType.MESH,
+                src_ref=mine.at[stage], dst_ref=others.at[k],
+                send_sem=give_sem.at[k], recv_sem=take_sem.at[k],
+                device_id=at(di, dx), device_id_type=pl.DeviceIdType.MESH,
             )
             copy.start()
             copies.append(copy)
-        total = source[...]
-        for copy in copies:
-            copy.wait_recv()
-        for k in range(count - 1):
+        for k in range(first, len(copies)):
+            copies[k].wait_recv()
             total = total + others[k]
-        return total, copies
-
-    total, copies_x = reduce(nx_dev, my_x, "xln", mine.at[0], others_x, xs_sem, xr_sem)
-    mine[1] = total
-    total, copies_i = reduce(ni_dev, my_i, "inl", mine.at[1], others_i, is_sem, ir_sem)
-    at = 2 * lax.broadcasted_iota(jnp.int32, (2, 2), 0) + lax.broadcasted_iota(jnp.int32, (2, 2), 1)
-    result = jnp.zeros((2, 2), jnp.float32)
-    for k in range(4):
-        result = jnp.where(at == k, jnp.sum(total[k : k + 1], keepdims=True), result)
-    norms[...] = jnp.sqrt(result)
-
-    for copy in copies_x + copies_i:
+    norms[...] = jnp.sqrt(jnp.concatenate([total, pltpu.roll(total, 126, 1)], axis=0)[:, 0:2])
+
+    for copy in copies:
         copy.wait_send()
     for copy, can_send in sent:
         @pl.when(can_send)
@@ -315,6 +346,8 @@
     slab = pltpu.VMEM((nx, nz), f32)
     dma = pltpu.SemaphoreType.DMA
     volume = 4 * ni * nx * nz
+    stages = reduction(ni_dev, nx_dev)
+    peers = sum(len(stage) for stage in stages)
     noisy = pltpu.with_memory_space_constraint(noisy, pltpu.HBM)
     bound = pltpu.with_memory_space_constraint(bound, pltpu.HBM)
     held = pl.pallas_call(
@@ -337,11 +370,9 @@
             slab,
             *([face] * 12),
             slab,
-            pltpu.VMEM((2, 4, 128), f32),
-            pltpu.VMEM((nx_dev - 1, 4, 128), f32),
-            pltpu.VMEM((ni_dev - 1, 4, 128), f32),
-            dma((5,)), dma((10,)), dma((10,)),
-            dma((nx_dev - 1,)), dma((nx_dev - 1,)), dma((ni_dev - 1,)), dma((ni_dev - 1,)),
+            pltpu.VMEM((len(stages), 1, 128), f32),
+            pltpu.VMEM((peers, 1, 128), f32),
+            dma((5,)), dma((10,)), dma((10,)), dma((peers,)), dma((peers,)),
         ],
         compiler_params=pltpu.CompilerParams(
             collective_id=0, has_side_effects=True, vmem_limit_bytes=24 * 1024 * 1024

time: 29.2 us -> 23.7 us (0.81)
  Pallas kernels: 28.4 us -> 22.9 us
    pallas_call x1, Pallas kernels: 25 us -> 19.5 us  [per_device(): pl.pallas_call(functools.partial(kernel, ni_dev, nx_dev), out_shape=(pltp...]
where the time goes in v1:
time: 23.7 us; the launch traced here: 23.5 us
  Pallas kernels  22.9 us (97%)
  between operations  0.64 us (3%)
    pallas_call x1, Pallas kernels, per_device(): pl.pallas_call(functools.partial(kernel, ni_dev, nx_dev), out_shape=(pltp...  19.5 us
    pallas_call x1, Pallas kernels, per_device(): pl.pallas_call(put_out, out_shape=(jax.ShapeDtypeStruct((ni, nx, nz), f32...  3.38 us

profile of v1, /device:TPU:0, one launch (start us, length us, event | category | flops | bytes accessed | tf_op | source)
XLA Modules:
  0.0 23.5 jit_solution(8594428407256984848)
XLA Ops:
  0.6 19.5 %denoise.1 = (f32[32,32,512]{2,1,0:T(8,128)S(1)}, f32[3,32,32,512]{3,2,1,0:T(8,128)S(1)}, f32[2,2]{1,0:T(2,128)S(1)}) custom-call(f32[32,32,512]{2,1,0:T(8,128)} %noisy.1, f32[32,32,512]{2,1,0:T(8,128)} %bound.1), custom_call_target="tpu_custom_call" | custom-call | flops 41943040 | bytes 12582912 | tf_op jit(solution)/shard_map/denoise/pallas_call | solution.py:353
  20.1 3.4 %put_out.1 = (f32[32,32,512]{2,1,0:T(8,128)}, f32[3,32,32,512]{3,2,1,0:T(8,128)}, f32[2,2]{1,0:T(2,128)}) custom-call(f32[32,32,512]{2,1,0:T(8,128)S(1)} %get-tuple-element.6.out_held, f32[3,32,32,512]{3,2,1,0:T(8,128)S(1)} %get-tuple-element.7.dual_held, f32[2,2]{1,0:T(2,128)S(1)} %get-tuple-element.8.norms_held), custom_call_target="tpu_custom_call" | custom-call | bytes 8388608 | tf_op jit(solution)/shard_map/put_out/pallas_call | solution.py:387

commit v2 on v1

--- a/solution.py
+++ b/solution.py
@@ -10,6 +10,9 @@
 SIGMA = 0.28
 TAU = 0.28
 GAIN = TAU / (1.0 + TAU)
+GROUP = 4
+MIDDLE = 7
+RIM = 7
 
 
 def clip(value, limit):
@@ -84,27 +87,17 @@
     ni_dev, nx_dev,
     noisy, bound, out, dual, norms,
     n, b, v, step,
-    nx_first, nx_last, bx_last, nx_next, nx_prev, bx_prev,
-    vx_first, vx_last, vx_next, vx_prev, dx_prev, dx_edge, di_prev,
+    nx_first, nx_last, bx_last, bx_first, nx_second, nx_semi, bx_semi,
+    nx_next, nx_prev, bx_prev,
+    vx_first, vx_last, vx_next, vx_prev, wx_first, wx_last, dx_prev, dx_edge,
+    zc_up, zc_down, zc_prev, zc_next, xc_up, xc_down, xc_prev, xc_next,
     mine, others,
-    load_sem, send_sem, recv_sem, give_sem, take_sem,
+    load_sem, chunk_sem, send_sem, recv_sem, give_sem, take_sem, far_sem,
 ):
     ni, nx, nz = noisy.shape
     top, end = ni, ni + 1
     my_i, my_x = lax.axis_index("inl"), lax.axis_index("xln")
-
-    loads = []
-
-    def load(src, dst):
-        copy = pltpu.make_async_copy(src, dst, load_sem.at[len(loads)])
-        copy.start()
-        loads.append(copy)
-
-    load(noisy.at[pl.ds(ni - 1, 1)], n.at[pl.ds(top, 1)])
-    load(bound.at[pl.ds(ni - 1, 1)], b.at[pl.ds(top, 1)])
-    load(noisy.at[pl.ds(0, 1)], n.at[pl.ds(1, 1)])
-    load(noisy.at[pl.ds(1, ni - 2)], n.at[pl.ds(2, ni - 2)])
-    load(bound.at[pl.ds(0, ni - 1)], b.at[pl.ds(1, ni - 1)])
+    f32 = jnp.float32
 
     barrier = pltpu.get_barrier_semaphore()
     stages = reduction(ni_dev, nx_dev)
@@ -115,7 +108,7 @@
     greeted = 0
     for di in range(1 - ni_dev, ni_dev):
         for dx in range(nx_dev):
-            if (di == 0 and dx == 0) or not (abs(di) <= 1 and (one_stage(ni_dev, nx_dev) or di * dx == 0) or (dx == 0 and not one_stage(ni_dev, nx_dev))):
+            if (di == 0 and dx == 0) or di * dx or (abs(di) > 1 and one_stage(ni_dev, nx_dev)):
                 continue
             exists = jnp.logical_and(my_i + di >= 0, my_i + di < ni_dev)
             greeted = greeted + exists.astype(jnp.int32)
@@ -127,11 +120,53 @@
                     device_id={"inl": my_i + di, "xln": lax.rem(my_x + dx, nx_dev)},
                     device_id_type=pl.DeviceIdType.MESH,
                 )
-    pl.semaphore_wait(barrier, greeted)
+
+    loads = []
+
+    def load(src, dst):
+        copy = pltpu.make_async_copy(src, dst, load_sem.at[len(loads)])
+        copy.start()
+        loads.append(copy)
+
+    load(noisy.at[:, 0, :], nx_first)
+    load(noisy.at[:, nx - 1, :], nx_last)
+    load(bound.at[:, nx - 1, :], bx_last)
+    load(bound.at[:, 0, :], bx_first)
+    load(noisy.at[pl.ds(ni - 1, 1)], n.at[pl.ds(top, 1)])
+    load(bound.at[pl.ds(ni - 1, 1)], b.at[pl.ds(top, 1)])
+    load(noisy.at[pl.ds(0, 1)], n.at[pl.ds(1, 1)])
+    load(noisy.at[:, 1, :], nx_second)
+    load(noisy.at[:, nx - 2, :], nx_semi)
+    load(bound.at[:, nx - 2, :], bx_semi)
+    def chunk(k, size):
+        return (
+            pltpu.make_async_copy(
+                noisy.at[pl.ds(GROUP * k + 1, size)], n.at[pl.ds(GROUP * k + 2, size)], chunk_sem.at[0, k]
+            ),
+            pltpu.make_async_copy(
+                bound.at[pl.ds(GROUP * k, size)], b.at[pl.ds(GROUP * k + 1, size)], chunk_sem.at[1, k]
+            ),
+        )
+
+    groups = (ni - 1) // GROUP
+    rest = ni - 1 - groups * GROUP
+    pieces = [(k, GROUP) for k in range(groups)]
+    tail = pltpu.make_async_copy(
+        bound.at[pl.ds(ni - 1 - rest, rest)], b.at[pl.ds(ni - rest, rest)], chunk_sem.at[1, groups]
+    )
+    tail_n = pltpu.make_async_copy(
+        noisy.at[pl.ds(ni - rest, rest - 1)], n.at[pl.ds(ni - rest + 1, rest - 1)], chunk_sem.at[0, groups]
+    )
+    for k, size in pieces:
+        for copy in chunk(k, size):
+            copy.start()
+    tail.start()
+    tail_n.start()
 
     sent = []
 
-    def send(slot, src, dst, axis, forward):
+    def send(src, dst, axis, forward):
+        slot = len(sent)
         me, count = (my_i, ni_dev) if axis == "inl" else (my_x, nx_dev)
         target = lax.rem(me + (1 if forward else count - 1), count)
         copy = pltpu.make_async_remote_copy(
@@ -158,26 +193,20 @@
 
         return arrive
 
+    def left(slot):
+        copy, can_send = sent[slot]
+
+        @pl.when(can_send)
+        def _():
+            copy.wait_send()
+
     def setter(dst, src):
         def fill():
             dst[...] = src[...]
 
         return fill
 
-    loads[0].wait()
-    got_n_prev = send(0, n.at[top], n.at[0], "inl", True)
-    loads[1].wait()
-    got_b_prev = send(1, b.at[top], b.at[0], "inl", True)
-    loads[2].wait()
-    got_n_next = send(2, n.at[1], n.at[end], "inl", False)
-    loads[3].wait()
-    nx_last[...] = n[1:end, nx - 1, :]
-    got_nx_prev = send(3, nx_last, nx_prev, "xln", True)
-    nx_first[...] = n[1:end, 0, :]
-    got_nx_next = send(5, nx_first, nx_next, "xln", False)
-    loads[4].wait()
-    bx_last[...] = b[1:end, nx - 1, :]
-    got_bx_prev = send(4, bx_last, bx_prev, "xln", True)
+    first, last = slice(0, 1), slice(ni - 1, ni)
 
     step[...] = jnp.zeros_like(step)
 
@@ -200,16 +229,171 @@
         return d1 + squares(di, dx, dz)
 
     zero = jnp.zeros((8, 128), jnp.float32)
-    d1 = stepped(0, ni - 1, pass_one, zero)
+
+    def pass_group(k, d1):
+        for copy in chunk(k, GROUP):
+            copy.wait()
+        for at in range(GROUP):
+            d1 = pass_one(GROUP * k + at, d1)
+        return d1
+
+    for k in range(10):
+        loads[k].wait()
+
+    def edge(here, limit, side):
+        di = clip(SIGMA * (ahead(here, 0) - here), limit)
+        dz = clip(SIGMA * (ahead(here, 1) - here), limit)
+        return here + (2.0 * GAIN) * ((di - behind(di, 0)) + side + (dz - behind(dz, 1)))
+
+    inward = clip(SIGMA * (nx_second[...] - nx_first[...]), bx_first[...])
+    vx_first[...] = edge(nx_first[...], bx_first[...], inward)
+    inward = clip(SIGMA * (nx_last[...] - nx_semi[...]), bx_semi[...])
+    vx_last[...] = edge(nx_last[...], bx_last[...], -inward)
+
+    early = 2
+    d1 = lax.fori_loop(0, early, pass_group, zero)
+    pl.semaphore_wait(barrier, greeted)
+    zc_up[0:1], zc_up[1:2], zc_up[2:3], zc_up[3:4] = nx_first[last], nx_last[last], bx_first[last], bx_last[last]
+    zc_down[0:1], zc_down[1:2] = nx_first[first], nx_last[first]
+    xc_up[0:1], xc_up[1:2], xc_up[2:3], xc_up[3:4] = nx_last[first], nx_last[last], bx_last[first], bx_last[last]
+    xc_down[0:1], xc_down[1:2] = nx_first[first], nx_first[last]
+    got_zc_prev = send(zc_up, zc_prev, "inl", True)
+    got_zc_next = send(zc_down, zc_next, "inl", False)
+    got_xc_prev = send(xc_up, xc_prev, "xln", True)
+    got_xc_next = send(xc_down, xc_next, "xln", False)
+    got_nx_prev = send(nx_last, nx_prev, "xln", True)
+    got_nx_next = send(nx_first, nx_next, "xln", False)
+    got_bx_prev = send(bx_last, bx_prev, "xln", True)
+    got_n_prev = send(n.at[top], n.at[0], "inl", True)
+    got_n_next = send(n.at[1], n.at[end], "inl", False)
+    got_b_prev = send(b.at[top], b.at[0], "inl", True)
+
+    tail.wait()
+    tail_n.wait()
     here, limit = n[top], b[top]
     dx = clip(SIGMA * (ahead(here, 0) - here), limit)
     dz = clip(SIGMA * (ahead(here, 1) - here), limit)
     dual[1, ni - 1] = dx
     dual[2, ni - 1] = dz
-    div = (dx - behind(dx, 0)) - step[...]
+    div = (dx - behind(dx, 0)) - clip(SIGMA * (here - n[top - 1]), b[top - 1])
     div = div + (dz - behind(dz, 1))
     v[top] = here + (2.0 * GAIN) * div
     d1 = d1 + fold(dx * dx + dz * dz)
+    d1 = lax.fori_loop(early, groups, pass_group, d1)
+    for i in range(groups * GROUP, ni - 1):
+        d1 = pass_one(i, d1)
+
+    def no_prev(dst):
+        def fill():
+            dst[...] = jnp.zeros_like(dst)
+
+        return fill
+
+    def no_next(dst, low, high):
+        def fill():
+            dst[0:1] = low
+            dst[1:2] = high
+
+        return fill
+
+    def grow(dst, rows, amount):
+        dst[rows] = dst[rows] + (2.0 * GAIN) * amount
+
+    got_zc_prev(no_prev(zc_prev))
+    got_zc_next(no_next(zc_next, nx_first[last], nx_last[last]))
+    grow(vx_first, first, -clip(SIGMA * (nx_first[first] - zc_prev[0:1]), zc_prev[2:3]))
+    grow(vx_last, first, -clip(SIGMA * (nx_last[first] - zc_prev[1:2]), zc_prev[3:4]))
+    grow(vx_first, last, clip(SIGMA * (zc_next[0:1] - nx_first[last]), bx_first[last]))
+    grow(vx_last, last, clip(SIGMA * (zc_next[1:2] - nx_last[last]), bx_last[last]))
+    got_vx_prev = send(vx_last, vx_prev, "xln", True)
+    got_vx_next = send(vx_first, vx_next, "xln", False)
+    got_xc_prev(no_prev(xc_prev))
+    got_xc_next(no_next(xc_next, nx_last[first], nx_last[last]))
+    for k, (rows, layer) in enumerate(((first, 1), (last, top))):
+        outer = clip(SIGMA * (xc_next[k : k + 1] - nx_last[rows]), bx_last[rows])
+        grow(v.at[layer], slice(nx - 1, nx), outer)
+        outer = clip(SIGMA * (nx_first[rows] - xc_prev[k : k + 1]), xc_prev[2 + k : 3 + k])
+        grow(v.at[layer], slice(0, 1), -outer)
+    v_up = len(sent)
+    got_v_prev = send(v.at[top], v.at[0], "inl", True)
+    v_down = len(sent)
+    got_v_next = send(v.at[1], v.at[end], "inl", False)
+
+    if one_stage(ni_dev, nx_dev):
+        for di in (2, -2):
+            beyond = my_i - di // 2
+            knows = jnp.logical_and(beyond >= 0, beyond < ni_dev)
+
+            @pl.when(jnp.logical_and(knows, jnp.logical_and(my_i + di >= 0, my_i + di < ni_dev)))
+            def _():
+                pl.semaphore_signal(
+                    far_sem, inc=1, device_id={"inl": my_i + di}, device_id_type=pl.DeviceIdType.MESH
+                )
+
+    row = lax.broadcasted_iota(jnp.int32, (8, nz), 0)
+
+    def inner_rows(value, lo, hi):
+        parts = split(value, 0, 8)
+        if lo == 0:
+            parts[0] = jnp.where(row == 0, 0.0, parts[0])
+        if hi == nx:
+            parts[-1] = jnp.where(row == 7, 0.0, parts[-1])
+        return jnp.concatenate(parts, axis=0)
+
+    def below(value, tile):
+        turned = [pltpu.roll(part, 7, 0) for part in split(value, 0, 8)]
+        over = [value[-8:] if tile is None else pltpu.roll(tile, 7, 0)]
+        return jnp.concatenate([jnp.where(row == 7, x, t) for x, t in zip(turned[1:] + over, turned)], axis=0)
+
+    def above(value, tile):
+        turned = [pltpu.roll(part, 1, 0) for part in split(value, 0, 8)]
+        under = [jnp.zeros_like(value[:8]) if tile is None else pltpu.roll(tile, 1, 0)]
+        return jnp.concatenate([jnp.where(row == 0, x, t) for x, t in zip(under + turned[:-1], turned)], axis=0)
+
+    def pass_two(i, so_far, lo=0, hi=nx, fresh=True):
+        p1, p2, d2 = so_far
+        here, limit, base = v[i + 1, lo:hi], b[i + 1, lo:hi], n[i + 1, lo:hi]
+        oi, ox, oz = dual[0, i, lo:hi], dual[1, i, lo:hi], dual[2, i, lo:hi]
+        di = clip(oi + SIGMA * (v[i + 2, lo:hi] - here), limit)
+        dx = clip(ox + SIGMA * (below(here, v[i + 1, hi : hi + 8] if hi < nx else None) - here), limit)
+        dz = clip(oz + SIGMA * (ahead(here, 1) - here), limit)
+        if lo == 0:
+            before = None
+        elif fresh:
+            before = v[i + 1, lo - 8 : lo]
+            before = clip(dual[1, i, lo - 8 : lo] + SIGMA * (below(before, here[:8]) - before), b[i + 1, lo - 8 : lo])
+        else:
+            before = dual[1, i, lo - 8 : lo]
+        dual[0, i, lo:hi] = di
+        dual[1, i, lo:hi] = dx
+        dual[2, i, lo:hi] = dz
+        div = di - step[lo:hi]
+        div = div + (dx - above(dx, before))
+        div = div + (dz - behind(dz, 1))
+        step[lo:hi] = di
+        half = 0.5 * (here - base)
+        change = GAIN * (div - half)
+        out[i, lo:hi] = base + half + change
+        inner = inner_rows(change, lo, hi)
+        return (
+            p1 + fold(half * half),
+            p2 + fold(inner * inner),
+            d2 + squares(di - oi, dx - ox, dz - oz),
+        )
+
+    def begin(lo, hi):
+        step[lo:hi] = clip(
+            dual[0, 1, lo:hi] + SIGMA * (v[3, lo:hi] - v[2, lo:hi]), b[2, lo:hi]
+        )
+
+    def middle(i, so_far):
+        return pass_two(i, so_far, 8, nx - 8)
+
+    def rim(i, so_far):
+        return pass_two(i, pass_two(i, so_far, 0, 8), nx - 8, nx, False)
+
+    begin(8, nx - 8)
+    sums = stepped(2, ni - 2, middle, (zero,) * 3, MIDDLE)
 
     got_nx_prev(setter(nx_prev, nx_first))
     got_bx_prev(setter(bx_prev, bx_last))
@@ -219,85 +403,67 @@
     dual[1, :, nx - 1, :] = dx_last
     dx_prev[...] = dxp
     dx_edge[...] = dx_last
-    v[1:end, nx - 1, :] = v[1:end, nx - 1, :] + (2.0 * GAIN) * dx_last
-    v[1:end, 0, :] = v[1:end, 0, :] - (2.0 * GAIN) * dxp
+    wx_last[...] = vx_last[...] + (2.0 * GAIN) * dx_last
+    wx_first[...] = vx_first[...] - (2.0 * GAIN) * dxp
+    v[2:top, nx - 1, :] = wx_last[1 : ni - 1]
+    v[2:top, 0, :] = wx_first[1 : ni - 1]
+    d1 = d1 + fold(dx_last * dx_last)
+
+    begin(0, 8)
+    begin(nx - 8, nx)
+    sums = stepped(2, ni - 2, rim, sums, RIM)
 
     got_n_prev(setter(n.at[0], n.at[1]))
     got_b_prev(setter(b.at[0], b.at[1]))
     got_n_next(setter(n.at[end], n.at[top]))
+    left(v_up)
+    left(v_down)
+    got_v_next(setter(v.at[end], v.at[top]))
+    got_v_prev(setter(v.at[0], v.at[1]))
     di_last = clip(SIGMA * (n[end] - n[top]), b[top])
     dip = clip(SIGMA * (n[1] - n[0]), b[0])
     dual[0, ni - 1] = di_last
-    di_prev[...] = dip
+    d1 = d1 + fold(di_last * di_last)
     v[top] = v[top] + (2.0 * GAIN) * di_last
     v[1] = v[1] - (2.0 * GAIN) * dip
-    got_v_prev = send(6, v.at[top], v.at[0], "inl", True)
-    got_v_next = send(7, v.at[1], v.at[end], "inl", False)
-    vx_last[...] = v[1:end, nx - 1, :]
-    got_vx_prev = send(8, vx_last, vx_prev, "xln", True)
-    vx_first[...] = v[1:end, 0, :]
-    got_vx_next = send(9, vx_first, vx_next, "xln", False)
-    d1 = d1 + fold(di_last * di_last) + fold(dx_last * dx_last)
-
-    row = lax.broadcasted_iota(jnp.int32, (8, nz), 0)
-
-    def inner_rows(value):
-        parts = split(value, 0, 8)
-        parts[0] = jnp.where(row == 0, 0.0, parts[0])
-        parts[-1] = jnp.where(row == 7, 0.0, parts[-1])
-        return jnp.concatenate(parts, axis=0)
-
-    def pass_two(i, sums):
-        p1, p2, d2 = sums
-        here, limit, base = v[i + 1], b[i + 1], n[i + 1]
-        oi, ox, oz = dual[0, i], dual[1, i], dual[2, i]
-        di = clip(oi + SIGMA * (v[i + 2] - here), limit)
-        dx = clip(ox + SIGMA * (ahead(here, 0) - here), limit)
-        dz = clip(oz + SIGMA * (ahead(here, 1) - here), limit)
-        dual[0, i] = di
-        dual[1, i] = dx
-        dual[2, i] = dz
-        div = di - step[...]
-        div = div + (dx - behind(dx, 0))
-        div = div + (dz - behind(dz, 1))
-        step[...] = di
-        half = 0.5 * (here - base)
-        change = GAIN * (div - half)
-        out[i] = base + half + change
-        inner = inner_rows(change)
-        return (
-            p1 + fold(half * half),
-            p2 + fold(inner * inner),
-            d2 + squares(di - oi, dx - ox, dz - oz),
-        )
-
-    step[...] = clip(dual[0, 0] + SIGMA * (v[2] - v[1]), b[1])
-    sums = stepped(1, ni - 1, pass_two, (zero,) * 3)
-
-    got_v_next(setter(v.at[end], v.at[top]))
+    v[end] = v[end] - (2.0 * GAIN) * di_last
+    v[0] = v[0] + (2.0 * GAIN) * dip
+    sums = pass_two(ni - 2, sums)
     sums = pass_two(ni - 1, sums)
-    got_v_prev(setter(v.at[0], v.at[1]))
-    step[...] = clip(di_prev[...] + SIGMA * (v[1] - v[0]), b[0])
-    p1, p2, d2 = pass_two(0, sums)
-
-    got_vx_prev(setter(vx_prev, vx_first))
-    got_vx_next(setter(vx_next, vx_last))
+    step[...] = clip(dip + SIGMA * (v[1] - v[0]), b[0])
+    sums = pass_two(0, sums)
+    p1, p2, d2 = pass_two(1, sums)
+
+    got_vx_prev(setter(vx_prev, wx_first))
+    got_vx_next(setter(vx_next, wx_last))
     was = dx_edge[...]
-    dx_last = clip(was + SIGMA * (vx_next[...] - vx_last[...]), bx_last[...])
+    dx_last = clip(
+        was + SIGMA * (vx_next[...] - (2.0 * GAIN) * was - wx_last[...]), bx_last[...]
+    )
     dual[1, :, nx - 1, :] = dx_last
     moved = dx_last - was
     d2 = d2 + fold(moved * moved)
     u_last = out[:, nx - 1, :] + GAIN * moved
     out[:, nx - 1, :] = u_last
-    dxp = clip(dx_prev[...] + SIGMA * (vx_first[...] - vx_prev[...]), bx_prev[...])
+    dxp = clip(
+        dx_prev[...] + SIGMA * (wx_first[...] - (vx_prev[...] + (2.0 * GAIN) * dx_prev[...])), bx_prev[...]
+    )
     u_first = out[:, 0, :] - GAIN * dxp
     out[:, 0, :] = u_first
-    change = u_last - (nx_last[...] + 0.5 * (vx_last[...] - nx_last[...]))
+    change = u_last - (nx_last[...] + 0.5 * (wx_last[...] - nx_last[...]))
     p2 = p2 + fold(change * change)
-    change = u_first - (nx_first[...] + 0.5 * (vx_first[...] - nx_first[...]))
+    change = u_first - (nx_first[...] + 0.5 * (wx_first[...] - nx_first[...]))
     p2 = p2 + fold(change * change)
 
     total = gather_lanes([jnp.sum(part, axis=0, keepdims=True) for part in (p1, d1, p2, d2)])
+    if one_stage(ni_dev, nx_dev):
+        far = 0
+        for di in (3, -3):
+            far = far + jnp.logical_and(my_i + di >= 0, my_i + di < ni_dev).astype(jnp.int32)
+        if ni_dev > 3:
+            @pl.when(far > 0)
+            def _():
+                pl.semaphore_wait(far_sem, 1)
     copies = []
     for stage, peers in enumerate(stages):
         mine[stage] = total
@@ -317,10 +483,9 @@
 
     for copy in copies:
         copy.wait_send()
-    for copy, can_send in sent:
-        @pl.when(can_send)
-        def _():
-            copy.wait_send()
+    for slot in range(len(sent)):
+        if slot not in (v_up, v_down):
+            left(slot)
 
 
 def put_out(out_held, dual_held, norms_held, out, dual, norms, sems):
@@ -368,11 +533,12 @@
             pltpu.VMEM((ni + 1, nx, nz), f32),
             pltpu.VMEM((ni + 2, nx, nz), f32),
             slab,
-            *([face] * 12),
-            slab,
+            *([face] * 18),
+            *([pltpu.VMEM((4, nz), f32), pltpu.VMEM((2, nz), f32)] * 4),
             pltpu.VMEM((len(stages), 1, 128), f32),
             pltpu.VMEM((peers, 1, 128), f32),
-            dma((5,)), dma((10,)), dma((10,)), dma((peers,)), dma((peers,)),
+            dma((10,)), dma((2, (ni - 1) // GROUP + 1)), dma((14,)), dma((14,)), dma((peers,)), dma((peers,)),
+            pltpu.SemaphoreType.REGULAR,
         ],
         compiler_params=pltpu.CompilerParams(
             collective_id=0, has_side_effects=True, vmem_limit_bytes=24 * 1024 * 1024

time: 23.7 us -> 22.6 us (0.954)
  Pallas kernels: 22.9 us -> 21.8 us
    pallas_call x1, Pallas kernels: 19.5 us -> 18.5 us  [per_device(): pl.pallas_call(functools.partial(kernel, ni_dev, nx_dev), out_shape=(pltp...]
where the time goes in v2:
time: 22.6 us; the launch traced here: 22.5 us
  Pallas kernels  21.8 us (96%)
  between operations  0.64 us (3%)
    pallas_call x1, Pallas kernels, per_device(): pl.pallas_call(functools.partial(kernel, ni_dev, nx_dev), out_shape=(pltp...  18.5 us
    pallas_call x1, Pallas kernels, per_device(): pl.pallas_call(put_out, out_shape=(jax.ShapeDtypeStruct((ni, nx, nz), f32...  3.38 us

profile of v2, /device:TPU:0, one launch (start us, length us, event | category | flops | bytes accessed | tf_op | source)
XLA Modules:
  0.0 22.5 jit_solution(3729835595356801729)
XLA Ops:
  0.6 18.5 %denoise.1 = (f32[32,32,512]{2,1,0:T(8,128)S(1)}, f32[3,32,32,512]{3,2,1,0:T(8,128)S(1)}, f32[2,2]{1,0:T(2,128)S(1)}) custom-call(f32[32,32,512]{2,1,0:T(8,128)} %noisy.1, f32[32,32,512]{2,1,0:T(8,128)} %bound.1), custom_call_target="tpu_custom_call" | custom-call | flops 41943040 | bytes 12582912 | tf_op jit(solution)/shard_map/denoise/pallas_call | solution.py:518
  19.1 3.4 %put_out.1 = (f32[32,32,512]{2,1,0:T(8,128)}, f32[3,32,32,512]{3,2,1,0:T(8,128)}, f32[2,2]{1,0:T(2,128)}) custom-call(f32[32,32,512]{2,1,0:T(8,128)S(1)} %get-tuple-element.6.out_held, f32[3,32,32,512]{3,2,1,0:T(8,128)S(1)} %get-tuple-element.7.dual_held, f32[2,2]{1,0:T(2,128)S(1)} %get-tuple-element.8.norms_held), custom_call_target="tpu_custom_call" | custom-call | bytes 8388608 | tf_op jit(solution)/shard_map/put_out/pallas_call | solution.py:553

commit v3 on v2

--- a/solution.py
+++ b/solution.py
@@ -11,6 +11,8 @@
 TAU = 0.28
 GAIN = TAU / (1.0 + TAU)
 GROUP = 4
+AHEAD = 1
+EARLY = 1
 MIDDLE = 7
 RIM = 7
 
@@ -30,11 +32,13 @@
     return part
 
 
-def gather_lanes(rows):
-    lane = lax.broadcasted_iota(jnp.int32, (1, 128), 1)
-    result = jnp.zeros((1, 128), jnp.float32)
-    for k, row in enumerate(rows):
-        result = jnp.where(lane == k, jnp.sum(row, axis=1, keepdims=True), result)
+def gather_lanes(parts):
+    lane = lax.broadcasted_iota(jnp.int32, (2, 128), 1)
+    row = lax.broadcasted_iota(jnp.int32, (2, 128), 0)
+    result = jnp.zeros((2, 128), jnp.float32)
+    for k, part in enumerate(parts):
+        total = jnp.sum(jnp.sum(part, axis=0, keepdims=True), axis=1, keepdims=True)
+        result = jnp.where(jnp.logical_and(row == k // 2, lane == k % 2), total, result)
     return result
 
 
@@ -89,7 +93,7 @@
     n, b, v, step,
     nx_first, nx_last, bx_last, bx_first, nx_second, nx_semi, bx_semi,
     nx_next, nx_prev, bx_prev,
-    vx_first, vx_last, vx_next, vx_prev, wx_first, wx_last, dx_prev, dx_edge,
+    vx_first, vx_last, vx_next, vx_prev, wx_first, wx_last, dx_prev, dx_edge, di_prev,
     zc_up, zc_down, zc_prev, zc_next, xc_up, xc_down, xc_prev, xc_next,
     mine, others,
     load_sem, chunk_sem, send_sem, recv_sem, give_sem, take_sem, far_sem,
@@ -105,21 +109,20 @@
     def at(di, dx):
         return {"inl": lax.rem(my_i + di, ni_dev), "xln": lax.rem(my_x + dx, nx_dev)}
 
+    hello = [(di, 0) for di in range(1 - ni_dev, ni_dev) if di and (abs(di) == 1 or not one_stage(ni_dev, nx_dev))]
+    hello = sorted(hello, key=lambda peer: abs(peer[0])) + [(0, dx) for dx in range(1, nx_dev)]
     greeted = 0
-    for di in range(1 - ni_dev, ni_dev):
-        for dx in range(nx_dev):
-            if (di == 0 and dx == 0) or di * dx or (abs(di) > 1 and one_stage(ni_dev, nx_dev)):
-                continue
-            exists = jnp.logical_and(my_i + di >= 0, my_i + di < ni_dev)
-            greeted = greeted + exists.astype(jnp.int32)
-
-            @pl.when(exists)
-            def _():
-                pl.semaphore_signal(
-                    barrier, inc=1,
-                    device_id={"inl": my_i + di, "xln": lax.rem(my_x + dx, nx_dev)},
-                    device_id_type=pl.DeviceIdType.MESH,
-                )
+    for di, dx in hello:
+        exists = jnp.logical_and(my_i + di >= 0, my_i + di < ni_dev)
+        greeted = greeted + exists.astype(jnp.int32)
+
+        @pl.when(exists)
+        def _():
+            pl.semaphore_signal(
+                barrier, inc=1,
+                device_id={"inl": my_i + di, "xln": lax.rem(my_x + dx, nx_dev)},
+                device_id_type=pl.DeviceIdType.MESH,
+            )
 
     loads = []
 
@@ -128,16 +131,6 @@
         copy.start()
         loads.append(copy)
 
-    load(noisy.at[:, 0, :], nx_first)
-    load(noisy.at[:, nx - 1, :], nx_last)
-    load(bound.at[:, nx - 1, :], bx_last)
-    load(bound.at[:, 0, :], bx_first)
-    load(noisy.at[pl.ds(ni - 1, 1)], n.at[pl.ds(top, 1)])
-    load(bound.at[pl.ds(ni - 1, 1)], b.at[pl.ds(top, 1)])
-    load(noisy.at[pl.ds(0, 1)], n.at[pl.ds(1, 1)])
-    load(noisy.at[:, 1, :], nx_second)
-    load(noisy.at[:, nx - 2, :], nx_semi)
-    load(bound.at[:, nx - 2, :], bx_semi)
     def chunk(k, size):
         return (
             pltpu.make_async_copy(
@@ -157,7 +150,20 @@
     tail_n = pltpu.make_async_copy(
         noisy.at[pl.ds(ni - rest, rest - 1)], n.at[pl.ds(ni - rest + 1, rest - 1)], chunk_sem.at[0, groups]
     )
-    for k, size in pieces:
+    load(noisy.at[pl.ds(0, 1)], n.at[pl.ds(1, 1)])
+    for k, size in pieces[:AHEAD]:
+        for copy in chunk(k, size):
+            copy.start()
+    load(noisy.at[:, 0, :], nx_first)
+    load(noisy.at[:, nx - 1, :], nx_last)
+    load(bound.at[:, nx - 1, :], bx_last)
+    load(bound.at[:, 0, :], bx_first)
+    load(noisy.at[pl.ds(ni - 1, 1)], n.at[pl.ds(top, 1)])
+    load(bound.at[pl.ds(ni - 1, 1)], b.at[pl.ds(top, 1)])
+    load(noisy.at[:, 1, :], nx_second)
+    load(noisy.at[:, nx - 2, :], nx_semi)
+    load(bound.at[:, nx - 2, :], bx_semi)
+    for k, size in pieces[AHEAD:]:
         for copy in chunk(k, size):
             copy.start()
     tail.start()
@@ -237,8 +243,26 @@
             d1 = pass_one(GROUP * k + at, d1)
         return d1
 
-    for k in range(10):
+    early = min(EARLY, groups)
+    loads[0].wait()
+    d1 = lax.fori_loop(0, early, pass_group, zero)
+    for k in range(1, 10):
         loads[k].wait()
+    zc_up[0:1], zc_up[1:2], zc_up[2:3], zc_up[3:4] = nx_first[last], nx_last[last], bx_first[last], bx_last[last]
+    zc_down[0:1], zc_down[1:2] = nx_first[first], nx_last[first]
+    xc_up[0:1], xc_up[1:2], xc_up[2:3], xc_up[3:4] = nx_last[first], nx_last[last], bx_last[first], bx_last[last]
+    xc_down[0:1], xc_down[1:2] = nx_first[first], nx_first[last]
+    pl.semaphore_wait(barrier, greeted)
+    got_zc_prev = send(zc_up, zc_prev, "inl", True)
+    got_zc_next = send(zc_down, zc_next, "inl", False)
+    got_xc_prev = send(xc_up, xc_prev, "xln", True)
+    got_xc_next = send(xc_down, xc_next, "xln", False)
+    got_n_prev = send(n.at[top], n.at[0], "inl", True)
+    got_n_next = send(n.at[1], n.at[end], "inl", False)
+    got_b_prev = send(b.at[top], b.at[0], "inl", True)
+    got_nx_prev = send(nx_last, nx_prev, "xln", True)
+    got_nx_next = send(nx_first, nx_next, "xln", False)
+    got_bx_prev = send(bx_last, bx_prev, "xln", True)
 
     def edge(here, limit, side):
         di = clip(SIGMA * (ahead(here, 0) - here), limit)
@@ -250,24 +274,7 @@
     inward = clip(SIGMA * (nx_last[...] - nx_semi[...]), bx_semi[...])
     vx_last[...] = edge(nx_last[...], bx_last[...], -inward)
 
-    early = 2
-    d1 = lax.fori_loop(0, early, pass_group, zero)
-    pl.semaphore_wait(barrier, greeted)
-    zc_up[0:1], zc_up[1:2], zc_up[2:3], zc_up[3:4] = nx_first[last], nx_last[last], bx_first[last], bx_last[last]
-    zc_down[0:1], zc_down[1:2] = nx_first[first], nx_last[first]
-    xc_up[0:1], xc_up[1:2], xc_up[2:3], xc_up[3:4] = nx_last[first], nx_last[last], bx_last[first], bx_last[last]
-    xc_down[0:1], xc_down[1:2] = nx_first[first], nx_first[last]
-    got_zc_prev = send(zc_up, zc_prev, "inl", True)
-    got_zc_next = send(zc_down, zc_next, "inl", False)
-    got_xc_prev = send(xc_up, xc_prev, "xln", True)
-    got_xc_next = send(xc_down, xc_next, "xln", False)
-    got_nx_prev = send(nx_last, nx_prev, "xln", True)
-    got_nx_next = send(nx_first, nx_next, "xln", False)
-    got_bx_prev = send(bx_last, bx_prev, "xln", True)
-    got_n_prev = send(n.at[top], n.at[0], "inl", True)
-    got_n_next = send(n.at[1], n.at[end], "inl", False)
-    got_b_prev = send(b.at[top], b.at[0], "inl", True)
-
+    d1 = lax.fori_loop(early, groups, pass_group, d1)
     tail.wait()
     tail_n.wait()
     here, limit = n[top], b[top]
@@ -279,7 +286,6 @@
     div = div + (dz - behind(dz, 1))
     v[top] = here + (2.0 * GAIN) * div
     d1 = d1 + fold(dx * dx + dz * dz)
-    d1 = lax.fori_loop(early, groups, pass_group, d1)
     for i in range(groups * GROUP, ni - 1):
         d1 = pass_one(i, d1)
 
@@ -418,24 +424,28 @@
     got_n_next(setter(n.at[end], n.at[top]))
     left(v_up)
     left(v_down)
-    got_v_next(setter(v.at[end], v.at[top]))
-    got_v_prev(setter(v.at[0], v.at[1]))
     di_last = clip(SIGMA * (n[end] - n[top]), b[top])
     dip = clip(SIGMA * (n[1] - n[0]), b[0])
     dual[0, ni - 1] = di_last
+    di_prev[...] = dip
     d1 = d1 + fold(di_last * di_last)
     v[top] = v[top] + (2.0 * GAIN) * di_last
     v[1] = v[1] - (2.0 * GAIN) * dip
-    v[end] = v[end] - (2.0 * GAIN) * di_last
-    v[0] = v[0] + (2.0 * GAIN) * dip
     sums = pass_two(ni - 2, sums)
-    sums = pass_two(ni - 1, sums)
-    step[...] = clip(dip + SIGMA * (v[1] - v[0]), b[0])
-    sums = pass_two(0, sums)
-    p1, p2, d2 = pass_two(1, sums)
+    step[...] = clip(dual[0, 0] + SIGMA * (v[2] - v[1]), b[1])
+    sums = pass_two(1, sums)
 
     got_vx_prev(setter(vx_prev, wx_first))
     got_vx_next(setter(vx_next, wx_last))
+    got_v_next(setter(v.at[end], v.at[top]))
+    got_v_prev(setter(v.at[0], v.at[1]))
+    v[end] = v[end] - (2.0 * GAIN) * dual[0, ni - 1]
+    v[0] = v[0] + (2.0 * GAIN) * di_prev[...]
+    step[...] = dual[0, ni - 2]
+    sums = pass_two(ni - 1, sums)
+    step[...] = clip(di_prev[...] + SIGMA * (v[1] - v[0]), b[0])
+    p1, p2, d2 = pass_two(0, sums)
+
     was = dx_edge[...]
     dx_last = clip(
         was + SIGMA * (vx_next[...] - (2.0 * GAIN) * was - wx_last[...]), bx_last[...]
@@ -455,7 +465,7 @@
     change = u_first - (nx_first[...] + 0.5 * (wx_first[...] - nx_first[...]))
     p2 = p2 + fold(change * change)
 
-    total = gather_lanes([jnp.sum(part, axis=0, keepdims=True) for part in (p1, d1, p2, d2)])
+    total = gather_lanes((p1, d1, p2, d2))
     if one_stage(ni_dev, nx_dev):
         far = 0
         for di in (3, -3):
@@ -464,25 +474,28 @@
             @pl.when(far > 0)
             def _():
                 pl.semaphore_wait(far_sem, 1)
-    copies = []
+    first = 0
+    waits = []
     for stage, peers in enumerate(stages):
         mine[stage] = total
-        first = len(copies)
         for k, (di, dx) in enumerate(peers, first):
-            copy = pltpu.make_async_remote_copy(
+            pltpu.make_async_remote_copy(
                 src_ref=mine.at[stage], dst_ref=others.at[k],
-                send_sem=give_sem.at[k], recv_sem=take_sem.at[k],
+                send_sem=give_sem.at[stage], recv_sem=take_sem.at[stage],
                 device_id=at(di, dx), device_id_type=pl.DeviceIdType.MESH,
-            )
-            copy.start()
-            copies.append(copy)
-        for k in range(first, len(copies)):
-            copies[k].wait_recv()
-            total = total + others[k]
-    norms[...] = jnp.sqrt(jnp.concatenate([total, pltpu.roll(total, 126, 1)], axis=0)[:, 0:2])
-
-    for copy in copies:
-        copy.wait_send()
+            ).start()
+        landed = others.at[pl.ds(first, len(peers))]
+        pltpu.make_async_copy(landed, landed, take_sem.at[stage]).wait()
+        waits.append(pltpu.make_async_copy(landed, landed, give_sem.at[stage]))
+        rows = [total] + [others[k] for k in range(first, first + len(peers))]
+        while len(rows) > 1:
+            rows = [sum(rows[k + 1 : k + 2], rows[k]) for k in range(0, len(rows), 2)]
+        total = rows[0]
+        first += len(peers)
+    norms[...] = jnp.sqrt(total[:, 0:2])
+
+    for copy in waits:
+        copy.wait()
     for slot in range(len(sent)):
         if slot not in (v_up, v_down):
             left(slot)
@@ -534,10 +547,11 @@
             pltpu.VMEM((ni + 2, nx, nz), f32),
             slab,
             *([face] * 18),
+            slab,
             *([pltpu.VMEM((4, nz), f32), pltpu.VMEM((2, nz), f32)] * 4),
-            pltpu.VMEM((len(stages), 1, 128), f32),
-            pltpu.VMEM((peers, 1, 128), f32),
-            dma((10,)), dma((2, (ni - 1) // GROUP + 1)), dma((14,)), dma((14,)), dma((peers,)), dma((peers,)),
+            pltpu.VMEM((len(stages), 2, 128), f32),
+            pltpu.VMEM((peers, 2, 128), f32),
+            dma((10,)), dma((2, (ni - 1) // GROUP + 1)), dma((14,)), dma((14,)), dma((len(stages),)), dma((len(stages),)),
             pltpu.SemaphoreType.REGULAR,
         ],
         compiler_params=pltpu.CompilerParams(

time: 22.6 us -> 21.4 us (0.947)
  Pallas kernels: 21.8 us -> 20.6 us
    pallas_call x1, Pallas kernels: 18.5 us -> 17.2 us  [per_device(): pl.pallas_call(functools.partial(kernel, ni_dev, nx_dev), out_shape=(pltp...]
where the time goes in v3:
time: 21.4 us; the launch traced here: 21.2 us
  Pallas kernels  20.6 us (96%)
  between operations  0.64 us (3%)
    pallas_call x1, Pallas kernels, per_device(): pl.pallas_call(functools.partial(kernel, ni_dev, nx_dev), out_shape=(pltp...  17.2 us
    pallas_call x1, Pallas kernels, per_device(): pl.pallas_call(put_out, out_shape=(jax.ShapeDtypeStruct((ni, nx, nz), f32...  3.38 us

profile of v3, /device:TPU:0, one launch (start us, length us, event | category | flops | bytes accessed | tf_op | source)
XLA Modules:
  0.0 21.2 jit_solution(8660657257048860631)
XLA Ops:
  0.6 17.2 %denoise.1 = (f32[32,32,512]{2,1,0:T(8,128)S(1)}, f32[3,32,32,512]{3,2,1,0:T(8,128)S(1)}, f32[2,2]{1,0:T(2,128)S(1)}) custom-call(f32[32,32,512]{2,1,0:T(8,128)} %noisy.1, f32[32,32,512]{2,1,0:T(8,128)} %bound.1), custom_call_target="tpu_custom_call" | custom-call | flops 41943040 | bytes 12582912 | tf_op jit(solution)/shard_map/denoise/pallas_call | solution.py:531
  17.8 3.4 %put_out.1 = (f32[32,32,512]{2,1,0:T(8,128)}, f32[3,32,32,512]{3,2,1,0:T(8,128)}, f32[2,2]{1,0:T(2,128)}) custom-call(f32[32,32,512]{2,1,0:T(8,128)S(1)} %get-tuple-element.6.out_held, f32[3,32,32,512]{3,2,1,0:T(8,128)S(1)} %get-tuple-element.7.dual_held, f32[2,2]{1,0:T(2,128)S(1)} %get-tuple-element.8.norms_held), custom_call_target="tpu_custom_call" | custom-call | bytes 8388608 | tf_op jit(solution)/shard_map/put_out/pallas_call | solution.py:567

commit v4 on v3

--- a/solution.py
+++ b/solution.py
@@ -47,7 +47,8 @@
 
 
 def reduction(ni_dev, nx_dev):
-    everyone = [(di, dx) for di in range(ni_dev) for dx in range(nx_dev) if di or dx]
+    around = [[*range(1, count), 0] for count in (ni_dev, nx_dev)]
+    everyone = [(di, dx) for di in around[0] for dx in around[1] if di or dx]
     if one_stage(ni_dev, nx_dev):
         return [everyone]
     return [[peer for peer in everyone if peer[0] == 0], [peer for peer in everyone if peer[1] == 0]]
@@ -109,21 +110,6 @@
     def at(di, dx):
         return {"inl": lax.rem(my_i + di, ni_dev), "xln": lax.rem(my_x + dx, nx_dev)}
 
-    hello = [(di, 0) for di in range(1 - ni_dev, ni_dev) if di and (abs(di) == 1 or not one_stage(ni_dev, nx_dev))]
-    hello = sorted(hello, key=lambda peer: abs(peer[0])) + [(0, dx) for dx in range(1, nx_dev)]
-    greeted = 0
-    for di, dx in hello:
-        exists = jnp.logical_and(my_i + di >= 0, my_i + di < ni_dev)
-        greeted = greeted + exists.astype(jnp.int32)
-
-        @pl.when(exists)
-        def _():
-            pl.semaphore_signal(
-                barrier, inc=1,
-                device_id={"inl": my_i + di, "xln": lax.rem(my_x + dx, nx_dev)},
-                device_id_type=pl.DeviceIdType.MESH,
-            )
-
     loads = []
 
     def load(src, dst):
@@ -154,6 +140,21 @@
     for k, size in pieces[:AHEAD]:
         for copy in chunk(k, size):
             copy.start()
+    hello = [(di, 0) for di in range(1 - ni_dev, ni_dev) if di and (abs(di) == 1 or not one_stage(ni_dev, nx_dev))]
+    hello = sorted(hello, key=lambda peer: abs(peer[0])) + [(0, dx) for dx in range(1, nx_dev)]
+    greeted = 0
+    for di, dx in hello:
+        exists = jnp.logical_and(my_i + di >= 0, my_i + di < ni_dev)
+        greeted = greeted + exists.astype(jnp.int32)
+
+        @pl.when(exists)
+        def _():
+            pl.semaphore_signal(
+                barrier, inc=1,
+                device_id={"inl": my_i + di, "xln": lax.rem(my_x + dx, nx_dev)},
+                device_id_type=pl.DeviceIdType.MESH,
+            )
+
     load(noisy.at[:, 0, :], nx_first)
     load(noisy.at[:, nx - 1, :], nx_last)
     load(bound.at[:, nx - 1, :], bx_last)
@@ -475,7 +476,6 @@
             def _():
                 pl.semaphore_wait(far_sem, 1)
     first = 0
-    waits = []
     for stage, peers in enumerate(stages):
         mine[stage] = total
         for k, (di, dx) in enumerate(peers, first):
@@ -485,20 +485,18 @@
                 device_id=at(di, dx), device_id_type=pl.DeviceIdType.MESH,
             ).start()
         landed = others.at[pl.ds(first, len(peers))]
-        pltpu.make_async_copy(landed, landed, take_sem.at[stage]).wait()
-        waits.append(pltpu.make_async_copy(landed, landed, give_sem.at[stage]))
+        if stage == 0:
+            for slot in range(len(sent)):
+                if slot not in (v_up, v_down):
+                    left(slot)
+        for sem in (give_sem, take_sem):
+            pltpu.make_async_copy(landed, landed, sem.at[stage]).wait()
         rows = [total] + [others[k] for k in range(first, first + len(peers))]
         while len(rows) > 1:
             rows = [sum(rows[k + 1 : k + 2], rows[k]) for k in range(0, len(rows), 2)]
         total = rows[0]
         first += len(peers)
     norms[...] = jnp.sqrt(total[:, 0:2])
-
-    for copy in waits:
-        copy.wait()
-    for slot in range(len(sent)):
-        if slot not in (v_up, v_down):
-            left(slot)
 
 
 def put_out(out_held, dual_held, norms_held, out, dual, norms, sems):

time: 21.4 us -> 21.2 us (level)
  no operation moved by 1% of the time
where the time goes in v4:
time: 21.2 us; the launch traced here: 21.1 us
  Pallas kernels  20.5 us (97%)
  between operations  0.64 us (3%)
    pallas_call x1, Pallas kernels, per_device(): pl.pallas_call(functools.partial(kernel, ni_dev, nx_dev), out_shape=(pltp...  17.1 us
    pallas_call x1, Pallas kernels, per_device(): pl.pallas_call(put_out, out_shape=(jax.ShapeDtypeStruct((ni, nx, nz), f32...  3.38 us

profile of v4, /device:TPU:0, one launch (start us, length us, event | category | flops | bytes accessed | tf_op | source)
XLA Modules:
  0.0 21.1 jit_solution(2032861626908867568)
XLA Ops:
  0.6 17.1 %denoise.1 = (f32[32,32,512]{2,1,0:T(8,128)S(1)}, f32[3,32,32,512]{3,2,1,0:T(8,128)S(1)}, f32[2,2]{1,0:T(2,128)S(1)}) custom-call(f32[32,32,512]{2,1,0:T(8,128)} %noisy.1, f32[32,32,512]{2,1,0:T(8,128)} %bound.1), custom_call_target="tpu_custom_call" | custom-call | flops 41943040 | bytes 12582912 | tf_op jit(solution)/shard_map/denoise/pallas_call | solution.py:529
  17.7 3.4 %put_out.1 = (f32[32,32,512]{2,1,0:T(8,128)}, f32[3,32,32,512]{3,2,1,0:T(8,128)}, f32[2,2]{1,0:T(2,128)}) custom-call(f32[32,32,512]{2,1,0:T(8,128)S(1)} %get-tuple-element.6.out_held, f32[3,32,32,512]{3,2,1,0:T(8,128)S(1)} %get-tuple-element.7.dual_held, f32[2,2]{1,0:T(2,128)S(1)} %get-tuple-element.8.norms_held), custom_call_target="tpu_custom_call" | custom-call | bytes 8388608 | tf_op jit(solution)/shard_map/put_out/pallas_call | solution.py:565

commit v5 on v4

--- a/solution.py
+++ b/solution.py
@@ -222,9 +222,10 @@
 
     def pass_one(i, d1):
         here, limit = n[i + 1], b[i + 1]
-        di = clip(SIGMA * (n[i + 2] - here), limit)
-        dx = clip(SIGMA * (ahead(here, 0) - here), limit)
-        dz = clip(SIGMA * (ahead(here, 1) - here), limit)
+        scaled = SIGMA * here
+        di = clip(SIGMA * n[i + 2] - scaled, limit)
+        dx = clip(ahead(scaled, 0) - scaled, limit)
+        dz = clip(ahead(scaled, 1) - scaled, limit)
         dual[0, i] = di
         dual[1, i] = dx
         dual[2, i] = dz
@@ -361,9 +362,10 @@
         p1, p2, d2 = so_far
         here, limit, base = v[i + 1, lo:hi], b[i + 1, lo:hi], n[i + 1, lo:hi]
         oi, ox, oz = dual[0, i, lo:hi], dual[1, i, lo:hi], dual[2, i, lo:hi]
-        di = clip(oi + SIGMA * (v[i + 2, lo:hi] - here), limit)
-        dx = clip(ox + SIGMA * (below(here, v[i + 1, hi : hi + 8] if hi < nx else None) - here), limit)
-        dz = clip(oz + SIGMA * (ahead(here, 1) - here), limit)
+        scaled = SIGMA * here
+        di = clip(oi + (SIGMA * v[i + 2, lo:hi] - scaled), limit)
+        dx = clip(ox + (below(scaled, SIGMA * v[i + 1, hi : hi + 8] if hi < nx else None) - scaled), limit)
+        dz = clip(oz + (ahead(scaled, 1) - scaled), limit)
         if lo == 0:
             before = None
         elif fresh:

time: 21.2 us -> 21.1 us (level)
  no operation moved by 1% of the time
where the time goes in v5:
time: 21.1 us; the launch traced here: 20.9 us
  Pallas kernels  20.3 us (96%)
  between operations  0.64 us (3%)
    pallas_call x1, Pallas kernels, per_device(): pl.pallas_call(functools.partial(kernel, ni_dev, nx_dev), out_shape=(pltp...  16.9 us
    pallas_call x1, Pallas kernels, per_device(): pl.pallas_call(put_out, out_shape=(jax.ShapeDtypeStruct((ni, nx, nz), f32...  3.38 us

profile of v5, /device:TPU:0, one launch (start us, length us, event | category | flops | bytes accessed | tf_op | source)
XLA Modules:
  0.0 20.9 jit_solution(13553275246569100875)
XLA Ops:
  0.6 16.9 %denoise.1 = (f32[32,32,512]{2,1,0:T(8,128)S(1)}, f32[3,32,32,512]{3,2,1,0:T(8,128)S(1)}, f32[2,2]{1,0:T(2,128)S(1)}) custom-call(f32[32,32,512]{2,1,0:T(8,128)} %noisy.1, f32[32,32,512]{2,1,0:T(8,128)} %bound.1), custom_call_target="tpu_custom_call" | custom-call | flops 41943040 | bytes 12582912 | tf_op jit(solution)/shard_map/denoise/pallas_call | solution.py:531
  17.6 3.4 %put_out.1 = (f32[32,32,512]{2,1,0:T(8,128)}, f32[3,32,32,512]{3,2,1,0:T(8,128)}, f32[2,2]{1,0:T(2,128)}) custom-call(f32[32,32,512]{2,1,0:T(8,128)S(1)} %get-tuple-element.6.out_held, f32[3,32,32,512]{3,2,1,0:T(8,128)S(1)} %get-tuple-element.7.dual_held, f32[2,2]{1,0:T(2,128)S(1)} %get-tuple-element.8.norms_held), custom_call_target="tpu_custom_call" | custom-call | bytes 8388608 | tf_op jit(solution)/shard_map/put_out/pallas_call | solution.py:567

commit v6 on v5

--- a/solution.py
+++ b/solution.py
@@ -13,7 +13,7 @@
 GROUP = 4
 AHEAD = 1
 EARLY = 1
-MIDDLE = 7
+MIDDLE = 14
 RIM = 7
 
 

time: 21.1 us -> 21.2 us (level)
  no operation moved by 1% of the time
where the time goes in v6:
time: 21.2 us; the launch traced here: 21.1 us
  Pallas kernels  20.4 us (96%)
  between operations  0.64 us (3%)
    pallas_call x1, Pallas kernels, per_device(): pl.pallas_call(functools.partial(kernel, ni_dev, nx_dev), out_shape=(pltp...  17 us
    pallas_call x1, Pallas kernels, per_device(): pl.pallas_call(put_out, out_shape=(jax.ShapeDtypeStruct((ni, nx, nz), f32...  3.38 us

profile of v6, /device:TPU:0, one launch (start us, length us, event | category | flops | bytes accessed | tf_op | source)
XLA Modules:
  0.0 21.1 jit_solution(7370743770512624379)
XLA Ops:
  0.6 17.0 %denoise.1 = (f32[32,32,512]{2,1,0:T(8,128)S(1)}, f32[3,32,32,512]{3,2,1,0:T(8,128)S(1)}, f32[2,2]{1,0:T(2,128)S(1)}) custom-call(f32[32,32,512]{2,1,0:T(8,128)} %noisy.1, f32[32,32,512]{2,1,0:T(8,128)} %bound.1), custom_call_target="tpu_custom_call" | custom-call | flops 41943040 | bytes 12582912 | tf_op jit(solution)/shard_map/denoise/pallas_call | solution.py:531
  17.7 3.4 %put_out.1 = (f32[32,32,512]{2,1,0:T(8,128)}, f32[3,32,32,512]{3,2,1,0:T(8,128)}, f32[2,2]{1,0:T(2,128)}) custom-call(f32[32,32,512]{2,1,0:T(8,128)S(1)} %get-tuple-element.6.out_held, f32[3,32,32,512]{3,2,1,0:T(8,128)S(1)} %get-tuple-element.7.dual_held, f32[2,2]{1,0:T(2,128)S(1)} %get-tuple-element.8.norms_held), custom_call_target="tpu_custom_call" | custom-call | bytes 8388608 | tf_op jit(solution)/shard_map/put_out/pallas_call | solution.py:567
